TPU v7x, 32 devices: a whole 2x2x4 slice. The times are simulated.
32 devices in a mesh: fsdp: 2 (over core), ctx: 4 (over y, x), tp: 4 (over z).
Axes of the slice: x: 2, y: 2, z: 4, core: 2. Of those that a mesh axis runs over, the one named last changes fastest.
Arguments:
- tokens_in: bfloat16 [4, 2048, 768], P(None, ('fsdp', 'ctx', 'tp')), may hold values from -6 to 6
- cotangent: bfloat16 [4, 2048, 768], P(None, ('fsdp', 'ctx', 'tp')), may hold values from -6 to 6
- seq_lengths: int32 [4, 2, 3], P(None, 'fsdp'), may hold values from 1 to 512, 1024 in all within a row
- row_order: int32 [4, 2, 1024], P(None, 'fsdp'), may hold values from 0 to 1023, each once within a row
- w_query: bfloat16 [768, 768], P(('fsdp', 'ctx'), 'tp'), may hold values from -0.3125 to 0.3125
- b_query: bfloat16 [12, 64], P('tp', ('fsdp', 'ctx')), may hold values from -3 to 3
- w_key: bfloat16 [768, 768], P(('fsdp', 'ctx'), 'tp'), may hold values from -0.3125 to 0.3125
- w_value: bfloat16 [768, 768], P(('fsdp', 'ctx'), 'tp'), may hold values from -0.21875 to 0.21875
- b_value: bfloat16 [12, 64], P('tp', ('fsdp', 'ctx')), may hold values from -3 to 3
- w_out: bfloat16 [768, 768], P(('fsdp', 'ctx'), 'tp'), may hold values from -1 to 1
- b_out: bfloat16 [768], P(('fsdp', 'ctx')), may hold values from -3 to 3
- mid_gain: bfloat16 [768], P(('fsdp', 'ctx')), may hold values from 0.099609375 to 1.8984375
- mid_shift: bfloat16 [768], P(('fsdp', 'ctx')), may hold values from -3 to 3
- w_up: bfloat16 [768, 3072], P(('fsdp', 'ctx'), 'tp'), may hold values from -0.21875 to 0.21875
- b_up: bfloat16 [12, 256], P('tp', ('fsdp', 'ctx')), may hold values from -3 to 3
- w_down: bfloat16 [768, 3072], P(('fsdp', 'ctx'), 'tp'), may hold values from -0.15625 to 0.15625
- b_down: bfloat16 [768], P(('fsdp', 'ctx')), may hold values from -3 to 3
- end_gain: bfloat16 [768], P(('fsdp', 'ctx')), may hold values from 0.099609375 to 1.8984375
- end_shift: bfloat16 [768], P(('fsdp', 'ctx')), may hold values from -3 to 3
Outputs:
- layer_out: bfloat16 [4, 2048, 768], P(None, ('fsdp', 'ctx', 'tp'))
- input_grad: bfloat16 [4, 2048, 768], P(None, ('fsdp', 'ctx', 'tp'))
- grad_w_query: float32 [768, 768], P(('fsdp', 'ctx'), 'tp')
- grad_b_query: float32 [12, 64], P('tp', ('fsdp', 'ctx'))
- grad_w_key: float32 [768, 768], P(('fsdp', 'ctx'), 'tp')
- grad_w_value: float32 [768, 768], P(('fsdp', 'ctx'), 'tp')
- grad_b_value: float32 [12, 64], P('tp', ('fsdp', 'ctx'))
- grad_w_out: float32 [768, 768], P(('fsdp', 'ctx'), 'tp')
- grad_b_out: float32 [768], P(('fsdp', 'ctx'))
- grad_mid_gain: float32 [768], P(('fsdp', 'ctx'))
- grad_mid_shift: float32 [768], P(('fsdp', 'ctx'))
- grad_w_up: float32 [768, 3072], P(('fsdp', 'ctx'), 'tp')
- grad_b_up: float32 [12, 256], P('tp', ('fsdp', 'ctx'))
- grad_w_down: float32 [768, 3072], P(('fsdp', 'ctx'), 'tp')
- grad_b_down: float32 [768], P(('fsdp', 'ctx'))
- grad_end_gain: float32 [768], P(('fsdp', 'ctx'))
- grad_end_shift: float32 [768], P(('fsdp', 'ctx'))
Inputs may be any that keep to these rules, and one draw needn't show every extreme that they name: `seq_lengths`: each row of 3 lengths sums to 1024, and its largest is exactly 512. `row_order`: each row holds every number of 0 to 1023 once.
All inputs are finite; a program needn't handle non-finite values.
Results may differ from a plain program's by a relative error of at most 0.02.
Values may be sent and summed in bfloat16 or wider, within the bound.
A program may use at most 128 MiB of HBM per device.

v0:
```python
import jax
import jax.numpy as jnp
from jax import lax
from jax.sharding import PartitionSpec as P

EPS = 1e-06
MASKED = -1e30
ALL = ("fsdp", "ctx", "tp")
ROWS = ("fsdp", "ctx")
BF = jnp.bfloat16
F32 = jnp.float32


def mm(a, b):
    return jnp.dot(a, b, preferred_element_type=F32)


def mm_rt(a, b):
    return lax.dot_general(a, b, (((1,), (1,)), ((), ())), preferred_element_type=F32)


def mm_lt(a, b):
    return lax.dot_general(a, b, (((0,), (0,)), ((), ())), preferred_element_type=F32)


def norm(u):
    centre = u - jnp.mean(u, axis=-1, keepdims=True)
    inv = lax.rsqrt(jnp.mean(centre * centre, axis=-1, keepdims=True) + EPS)
    return (centre * inv, inv)


def norm_back(d, gain, n, inv):
    e = d * gain
    return (
        e - jnp.mean(e, axis=-1, keepdims=True) - n * jnp.mean(e * n, axis=-1, keepdims=True)
    ) * inv


def phi_both(u):
    cdf = 0.5 * (1.0 + lax.erf(u * 0.7071067811865476))
    pdf = 0.3989422804014327 * jnp.exp(-0.5 * u * u)
    return (cdf, pdf)


def gather_group(block):
    width = block.shape[-1]
    mine = lax.all_to_all(block, "ctx", 0, 0, tiled=True)
    whole = lax.all_gather(mine, "tp", axis=1, tiled=False)
    return whole.reshape(-1, width)


def scatter_group(rows, own_rows):
    ctx_n, tp_n = (lax.axis_size("ctx"), lax.axis_size("tp"))
    width = rows.shape[-1]
    blocks = rows.reshape(ctx_n, tp_n * own_rows, width)
    mine = lax.psum_scatter(blocks, "tp", scatter_dimension=1, tiled=True)
    return lax.all_to_all(mine, "ctx", 0, 0, tiled=True)


def body(
    tokens_in,
    cotangent,
    seq_lengths,
    row_order,
    w_query,
    b_query,
    w_key,
    w_value,
    b_value,
    w_out,
    b_out,
    mid_gain,
    mid_shift,
    w_up,
    b_up,
    w_down,
    b_down,
    end_gain,
    end_shift,
):
    ctx_n, tp_n, fsdp_n = (lax.axis_size("ctx"), lax.axis_size("tp"), lax.axis_size("fsdp"))
    rows_n = ctx_n * fsdp_n
    c, t = (lax.axis_index("ctx"), lax.axis_index("tp"))
    micro, own_rows, width = tokens_in.shape
    group_rows = own_rows * ctx_n * tp_n
    half_rows = group_rows // 2
    parts = tp_n // 2
    my_rows = half_rows // parts
    half, quarter = (t // parts, t % parts)
    heads_l, head_l = b_query.shape
    heads, head = (heads_l * tp_n, head_l * rows_n)
    mats = (w_query, w_key, w_value, w_out, w_up, w_down)
    widths = [m.shape[1] for m in mats]
    packed = lax.all_gather(jnp.concatenate(mats, axis=1), ALL, axis=0, tiled=False)
    full, at = ([], 0)
    for wd in widths:
        piece = packed[:, :, at : at + wd].reshape(rows_n, tp_n, -1, wd)
        full.append(piece.transpose(0, 2, 1, 3).reshape(width, tp_n * wd))
        at += wd
    wq, wk, wv, wo, wu, wd_ = full
    vecs = (b_out, mid_gain, mid_shift, b_down, end_gain, end_shift)
    bias = (b_query, b_value, b_up)
    vec_all = lax.all_gather(jnp.stack(vecs), ROWS, axis=1, tiled=True).astype(F32)
    bias_all = lax.all_gather(jnp.concatenate(bias, axis=1), ALL, axis=0, tiled=False).astype(F32)

    def whole_bias(at, wd):
        piece = bias_all[:, :, at : at + wd].reshape(rows_n, tp_n, heads_l, wd)
        return piece.transpose(1, 2, 0, 3).reshape(-1)

    bq = whole_bias(0, head_l)
    bv = whole_bias(head_l, head_l)
    bu = whole_bias(2 * head_l, b_up.shape[1])
    bo, mg, ms, bd, eg, es = (vec_all[i] for i in range(6))
    lens = lax.dynamic_index_in_dim(seq_lengths[:, 0], c, 0, keepdims=False)
    order = lax.dynamic_index_in_dim(row_order[:, 0], c, 0, keepdims=False)
    places = lax.iota(jnp.int32, lens.shape[0])
    longest = jnp.argmax(lens)
    first = jnp.sum(jnp.where(places < longest, lens, 0))
    start = lax.rem(first + half * half_rows, group_rows)
    ends = jnp.cumsum(lens)
    nat = lax.rem(start + lax.iota(jnp.int32, half_rows), group_rows)
    seg = jnp.sum((ends[None, :] <= nat[:, None]).astype(jnp.int32), axis=1)
    q_at = quarter * my_rows
    nat_q = lax.dynamic_slice_in_dim(nat, q_at, my_rows)
    seg_q = lax.dynamic_slice_in_dim(seg, q_at, my_rows)
    x_group = gather_group(tokens_in)
    c_group = gather_group(cotangent)
    x_twice = jnp.concatenate([x_group, x_group[:half_rows]], axis=0)
    x_half = lax.dynamic_slice_in_dim(x_twice, start, half_rows, 0)
    x_mine = lax.dynamic_slice_in_dim(x_half, q_at, my_rows, 0)
    pick = (order[:, None] == nat_q[None, :]).astype(BF)
    pick_nat = (lax.iota(jnp.int32, group_rows)[:, None] == nat_q[None, :]).astype(BF)
    dy = mm_lt(pick, c_group)
    x = x_mine.astype(F32)
    q = (mm(x_mine, wq) + bq).astype(BF).reshape(my_rows, heads, head)
    k = mm(x_half, wk).astype(BF).reshape(half_rows, heads, head)
    v = (mm(x_half, wv) + bv).astype(BF).reshape(half_rows, heads, head)
    same = seg_q[:, None] == seg[None, :]
    s = jnp.einsum("qhd,khd->hqk", q, k, preferred_element_type=F32) * 0.125
    s = jnp.where(same[None], s, MASKED)
    p = jnp.exp(s - jnp.max(s, axis=-1, keepdims=True))
    p = p / jnp.sum(p, axis=-1, keepdims=True)
    pb = p.astype(BF)
    o = jnp.einsum("hqk,khd->qhd", pb, v, preferred_element_type=F32).astype(BF)
    o2 = o.reshape(my_rows, heads * head)
    r1 = x + mm_rt(o2, wo) + bo
    n1, inv1 = norm(r1)
    middle = n1 * mg + ms
    mid_b = middle.astype(BF)
    pre = mm(mid_b, wu) + bu
    cdf, pdf = phi_both(pre)
    act = (pre * cdf).astype(BF)
    r2 = middle + mm_rt(act, wd_) + bd
    n2, inv2 = norm(r2)
    y = n2 * eg + es
    d_r2 = norm_back(dy, eg, n2, inv2)
    df = d_r2.astype(BF)
    d_pre = (mm(df, wd_) * (cdf + pre * pdf)).astype(BF)
    g_down = mm_lt(df, act)
    g_up = mm_lt(mid_b, d_pre)
    d_mid = d_r2 + mm_rt(d_pre, wu)
    d_r1 = norm_back(d_mid, mg, n1, inv1)
    da = d_r1.astype(BF)
    g_out = mm_lt(da, o2)
    d_o = mm(da, wo).astype(BF).reshape(my_rows, heads, head)
    dp = jnp.einsum("qhd,khd->hqk", d_o, v, preferred_element_type=F32)
    ds = (p * (dp - jnp.sum(p * dp, axis=-1, keepdims=True))).astype(BF)
    d_q = (jnp.einsum("hqk,khd->qhd", ds, k, preferred_element_type=F32) * 0.125).astype(BF)
    d_k = jnp.einsum("hqk,qhd->khd", ds, q, preferred_element_type=F32) * 0.125
    d_v = jnp.einsum("hqk,qhd->khd", pb, d_o, preferred_element_type=F32)
    d_q = d_q.reshape(my_rows, heads * head)
    d_kv = jnp.concatenate([d_k.reshape(half_rows, -1), d_v.reshape(half_rows, -1)], axis=1).astype(
        BF
    )
    pairs = [[h * parts + j for j in range(parts)] for h in range(tp_n // parts)]
    d_kv = lax.psum_scatter(
        d_kv.astype(F32), "tp", scatter_dimension=0, tiled=True, axis_index_groups=pairs
    )
    d_k, d_v = jnp.split(d_kv.astype(BF), 2, axis=1)
    g_q = mm_lt(x_mine, d_q)
    g_k = mm_lt(x_mine, d_k)
    g_v = mm_lt(x_mine, d_v)
    d_x = (d_r1 + mm_rt(d_q, wq) + mm_rt(d_k, wk) + mm_rt(d_v, wv)).astype(BF)
    layer_out = scatter_group(mm(pick, y.astype(BF)).astype(BF), own_rows)
    input_grad = scatter_group(mm(pick_nat, d_x).astype(BF), own_rows)
    outs = []
    for g, wd in zip((g_q, g_k, g_v, g_out, g_up, g_down), widths):
        outs.append(g.astype(BF).reshape(rows_n, width // rows_n, tp_n, wd).transpose(0, 2, 1, 3))
    packed_g = jnp.concatenate(outs, axis=3)
    packed_g = packed_g.reshape(rows_n * tp_n, width // rows_n, -1)
    mine_g = lax.psum_scatter(packed_g, ALL, scatter_dimension=0, tiled=True)[0].astype(F32)
    gm, at = ([], 0)
    for wd in widths:
        gm.append(mine_g[:, at : at + wd])
        at += wd

    def total(a):
        return jnp.sum(a.astype(F32), axis=0)

    def split_bias(a, wd):
        return (
            a.reshape(tp_n, heads_l, rows_n, wd)
            .transpose(2, 0, 1, 3)
            .reshape(rows_n * tp_n, heads_l, wd)
        )

    small_b = jnp.concatenate(
        [
            split_bias(total(d_q), head_l),
            split_bias(total(d_v), head_l),
            split_bias(total(d_pre), b_up.shape[1]),
        ],
        axis=2,
    ).reshape(rows_n * tp_n, -1)
    vec_g = jnp.stack(
        [total(d_r1), total(d_mid * n1), total(d_mid), total(d_r2), total(dy * n2), total(dy)]
    )
    small_v = vec_g.reshape(6, rows_n, 1, width // rows_n).transpose(1, 2, 0, 3)
    small_v = jnp.broadcast_to(small_v, (rows_n, tp_n, 6, width // rows_n)).reshape(
        rows_n * tp_n, -1
    )
    small = jnp.concatenate([small_b, small_v], axis=1)
    small = lax.psum_scatter(small, ALL, scatter_dimension=0, tiled=True)[0]
    nb = small_b.shape[1]
    sb = small[:nb].reshape(heads_l, -1)
    sv = small[nb:].reshape(6, -1)
    return (
        layer_out,
        input_grad,
        gm[0],
        sb[:, :head_l],
        gm[1],
        gm[2],
        sb[:, head_l : 2 * head_l],
        gm[3],
        sv[0],
        sv[1],
        sv[2],
        gm[4],
        sb[:, 2 * head_l :],
        gm[5],
        sv[3],
        sv[4],
        sv[5],
    )


def specs():
    tok = P(None, ALL, None)
    grp = P(None, "fsdp", None)
    mat = P(ROWS, "tp")
    bias = P("tp", ROWS)
    vec = P(ROWS)
    ins = (
        tok,
        tok,
        grp,
        grp,
        mat,
        bias,
        mat,
        mat,
        bias,
        mat,
        vec,
        vec,
        vec,
        mat,
        bias,
        mat,
        vec,
        vec,
        vec,
    )
    return (ins, (tok, tok) + ins[4:])


def solution(mesh):
    ins, outs = specs()
    return jax.shard_map(body, mesh=mesh, in_specs=ins, out_specs=outs, check_vma=False)
```

profile of v0, /device:TPU:0, one launch (start us, length us, event | category | flops | bytes accessed | tf_op | source)
XLA Modules:
  0.0 708.5 jit_solution(12837532554560193029)
XLA Ops:
  7.4 13.0 %all_to_all.20 = bf16[4,64,768]{2,1,0:T(8,128)(2,1)} all-to-all(bf16[4,64,768]{2,1,0:T(8,128)(2,1)} %param.19), channel_id=1, replica_groups=mesh['fsdp'=2,'ctx'=4,'tp'=4] {'ctx'}, dimensions={0} | all-to-all | bytes 786432 | tf_op jit(solution)/shard_map/all_to_all | solution.py:47
  29.6 21.1 %all-gather.5 = bf16[8,96,6]{1,2,0:T(8,128)(2,1)S(1)} all-gather(bf16[1,96,6]{1,2,0:T(8,128)(2,1)S(1)} %bitcast.231), channel_id=1, replica_groups=mesh['fsdp'=2,'ctx'=4,'tp'=4] {'fsdp','ctx'}, dimensions={0}, use_global_device_ids=true | all-gather | bytes 10368 | tf_op jit(solution)/shard_map/all_gather | solution.py:103
  50.9 68.8 %all-gather.4 = bf16[32,3,48]{2,1,0:T(4,128)(2,1)S(1)} all-gather(bf16[1,3,48]{2,1,0:T(4,128)(2,1)S(1)} %maximum_bitcast_fusion), channel_id=4, replica_groups=mesh['fsdp'=2,'ctx'=4,'tp'=4] {'fsdp','ctx','tp'}, dimensions={0}, use_global_device_ids=true | all-gather | bytes 9504 | tf_op jit(solution)/shard_map/all_gather | solution.py:104
  128.7 33.1 %all-gather.12.cloned.1.call-done = bf16[3072,2304]{1,0:T(8,128)(2,1)} async-done(((bf16[96,2304]{1,0:T(8,128)(2,1)}), bf16[3072,2304]{1,0:T(8,128)(2,1)}) %all-gather.12.cloned.1.call-update) | async-done | bytes 14155792 | tf_op jit(solution)/shard_map/all_gather | solution.py:94
  161.9 8.1 %fusion.61 = (bf16[32,96,768]{2,1,0:T(8,128)(2,1)}, bf16[32,96,768]{2,1,0:T(8,128)(2,1)}) fusion(bf16[32,96,2304]{2,1,0:T(8,128)(2,1)} %bitcast.177), kind=kLoop, calls=%fused_computation.141 | loop fusion | bytes 18874368 | tf_op jit(solution)/shard_map/slice | solution.py:97
  170.0 7.0 fusion.62
  216.3 6.1 fusion.67
  234.0 14.7 %copy.123 = bf16[8,96,4,768]{3,2,1,0:T(4,128)(2,1)S(1)} copy(bf16[8,96,4,768]{3,1,2,0:T(8,128)(2,1)S(1)} %bitcast.173) | data formatting | bytes 9437184 | tf_op jit(solution)/shard_map/transpose | solution.py:98
  259.9 5.0 convert_reduce_fusion
  306.3 19.4 %reduce-scatter.7.cloned.1.call-done = f32[256,1536]{0,1:T(8,128)} async-done(((f32[512,1536]{0,1:T(8,128)}), f32[256,1536]{0,1:T(8,128)}) %reduce-scatter.7.cloned.1.call-update) | async-done | bytes 1572880 | tf_op jit(solution)/shard_map/reduce_scatter | solution.py:176
  335.7 4.4 reshape.344
  341.8 4.4 reshape.347
  346.2 5.2 convolution_convert_fusion.1
  351.4 9.9 %reshape.348 = bf16[8,96,4,768]{3,2,1,0:T(4,128)(2,1)} reshape(bf16[768,3072]{1,0:T(8,128)(2,1)} %convolution_convert_fusion.1) | data formatting | bytes 9437184 | tf_op jit(solution)/shard_map/reshape | solution.py:188
  365.0 9.8 %reshape.349 = bf16[8,96,4,768]{3,2,1,0:T(4,128)(2,1)} reshape(bf16[768,3072]{1,0:T(8,128)(2,1)} %convolution_convert_fusion) | data formatting | bytes 9437184 | tf_op jit(solution)/shard_map/reshape | solution.py:188
  376.3 4.5 reshape.345
  382.4 4.8 reshape.346
  387.2 41.3 %concatenate.27 = bf16[8,4,96,2304]{3,1,2,0:T(4,128)(2,1)} concatenate(bf16[8,4,96,192]{3,1,2,0:T(4,128)(2,1)S(1)} %bitcast.179, bf16[8,4,96,192]{3,1,2,0:T(4,128)(2,1)} %bitcast.181, bf16[8,4,96,192]{3,1,2,0:T(4,128)(2,1)} %bitcast.182, bf16[8,4,96,192]{3,1,2,0:T(4,128)(2,1)S(1)} %bitcast.180, bf16[8,4,96,768]{3,1,2,0:T(4,128)(2,1)} %bitcast.167, bf16[8,4,96,768]{3,1,2,0:T(4,128)(2,1)} %bitcast.168), dimensions={3} | concatenate | bytes 28311552 | tf_op jit(solution)/shard_map/concatenate | solution.py:189
  428.5 11.3 %copy.125 = bf16[8,4,96,2304]{3,2,1,0:T(8,128)(2,1)} copy(bf16[8,4,96,2304]{3,1,2,0:T(4,128)(2,1)} %concatenate.27) | data formatting | bytes 28311552 | tf_op jit(solution)/shard_map/concatenate | solution.py:189
  443.5 6.5 all-to-all-done.1
  450.0 40.8 %all-reduce.3.cloned.1.call-done = f32[32,720]{1,0:T(8,128)} async-done(((f32[32,720]{1,0:T(8,128)}), f32[32,720]{1,0:T(8,128)}) %all-reduce.3.cloned.1.call-update) | async-done | bytes 92176
  492.3 37.2 %reduce-scatter.9.cloned.1.call-done = bf16[4,64,768]{2,1,0:T(8,128)(2,1)} async-done(((bf16[4,256,768]{2,1,0:T(8,128)(2,1)}), bf16[4,64,768]{2,1,0:T(8,128)(2,1)}) %reduce-scatter.9.cloned.1.call-update) | async-done | bytes 393232 | tf_op jit(solution)/shard_map/reduce_scatter | solution.py:56
  535.2 4.1 all-to-all-done.3
  539.4 157.6 %reduce-scatter.11.cloned.1.call-done = bf16[1,96,2304]{2,1,0:T(8,128)(2,1)} async-done(((bf16[32,96,2304]{2,1,0:T(8,128)(2,1)}), bf16[1,96,2304]{2,1,0:T(8,128)(2,1)}) %reduce-scatter.11.cloned.1.call-update) | async-done | bytes 442384 | tf_op jit(solution)/shard_map/reduce_scatter | solution.py:191
  (266 shorter events, 153.8 us)
Async XLA Ops:
  7.2 115.8 %copy-start = (s32[4,1,1024]{2,1,0:T(1,128)S(1)}, s32[4,1,1024]{2,1,0:T(1,128)}, u32[]{:S(2)}) copy-start(s32[4,1,1024]{2,1,0:T(1,128)} %param.22) | copy-start | bytes 49156
  7.2 22.3 %copy-start.54 = (bf16[96]{0:T(256)(128)(2,1)S(1)}, bf16[96]{0:T(256)(128)(2,1)}, u32[]{:S(2)}) copy-start(bf16[96]{0:T(256)(128)(2,1)} %param.29) | copy-start | bytes 580
  7.2 22.3 %copy-start.55 = (bf16[96]{0:T(256)(128)(2,1)S(1)}, bf16[96]{0:T(256)(128)(2,1)}, u32[]{:S(2)}) copy-start(bf16[96]{0:T(256)(128)(2,1)} %param.30) | copy-start | bytes 580
  7.2 22.3 %copy-start.56 = (bf16[96]{0:T(256)(128)(2,1)S(1)}, bf16[96]{0:T(256)(128)(2,1)}, u32[]{:S(2)}) copy-start(bf16[96]{0:T(256)(128)(2,1)} %param.31) | copy-start | bytes 580
  7.3 43.5 %copy-start.51 = (bf16[3,32]{1,0:T(4,128)(2,1)S(1)}, bf16[3,32]{1,0:T(4,128)(2,1)}, u32[]{:S(2)}) copy-start(bf16[3,32]{1,0:T(4,128)(2,1)} %param.33) | copy-start | bytes 580
  7.3 43.5 %copy-start.52 = (bf16[3,8]{1,0:T(4,128)(2,1)S(1)}, bf16[3,8]{1,0:T(4,128)(2,1)}, u32[]{:S(2)}) copy-start(bf16[3,8]{1,0:T(4,128)(2,1)} %param.27) | copy-start | bytes 148
  7.3 43.5 %copy-start.53 = (bf16[3,8]{1,0:T(4,128)(2,1)S(1)}, bf16[3,8]{1,0:T(4,128)(2,1)}, u32[]{:S(2)}) copy-start(bf16[3,8]{1,0:T(4,128)(2,1)} %param.24) | copy-start | bytes 148
  7.3 117.9 %all-gather.10.cloned.1.call-start = ((), (), s32[]{:S(2)}) async-start(), calls=%async_computation.12 | async-start | bytes 1966080 | tf_op jit(solution)/shard_map/all_gather | solution.py:48
  20.4 141.5 %all-gather.12.cloned.1.call-start = ((), (), s32[]{:S(2)}) async-start(), calls=%async_computation.13 | async-start | bytes 14598144 | tf_op jit(solution)/shard_map/all_gather | solution.py:94
  22.4 101.9 %all-to-all-start.2 = ((bf16[4,64,768]{2,1,0:T(8,128)(2,1)}), bf16[4,64,768]{2,1,0:T(8,128)(2,1)S(1)}, u32[]{:S(2)}, u32[]{:S(2)}) async-start(bf16[4,64,768]{2,1,0:T(8,128)(2,1)} %param.20), calls=%async_computation.3 | async-start | bytes 786432 | tf_op jit(solution)/shard_map/all_to_all | solution.py:47
  25.9 229.8 %all-gather.14.cloned.1.call-start = ((), (), s32[]{:S(2)}) async-start(), calls=%async_computation.14 | async-start | bytes 1966080 | tf_op jit(solution)/shard_map/all_gather | solution.py:48
  125.1 200.6 %reduce-scatter.7.cloned.1.call-start = ((), (), s32[]{:S(2)}) async-start(), calls=%async_computation.9 | async-start | bytes 4718592 | tf_op jit(solution)/shard_map/reduce_scatter | solution.py:176
  227.2 40.0 %copy-start.2 = (f32[256,768]{1,0:T(8,128)}, f32[256,768]{1,0:T(8,128)S(1)}, u32[]{:S(2)}) copy-start(f32[256,768]{1,0:T(8,128)S(1)} %get-tuple-element.62) | copy-start | bytes 2359300
  283.5 156.4 %reduce-scatter.5.cloned.1.call-start = ((), (), s32[]{:S(2)}) async-start(), calls=%async_computation.8 | async-start | bytes 1966080 | tf_op jit(solution)/shard_map/reduce_scatter | solution.py:56
  286.7 204.1 %all-reduce.3.cloned.1.call-start = ((), (), s32[]{:S(2)}) async-start(), calls=%async_computation.15 | async-start | bytes 196608
  303.9 23.6 %copy-start.29 = (f32[8,4,3,32]{3,1,0,2:T(4,128)S(1)}, f32[8,4,3,32]{3,1,0,2:T(4,128)}, u32[]{:S(2)}) copy-start(f32[8,4,3,32]{3,1,0,2:T(4,128)} %copy.128) | copy-start | bytes 36868
  304.0 23.7 %copy-start.28 = (f32[32,576]{1,0:T(8,128)S(1)}, f32[32,576]{1,0:T(8,128)}, u32[]{:S(2)}) copy-start(f32[32,576]{1,0:T(8,128)} %reshape.358) | copy-start | bytes 221188
  304.0 24.4 %copy-start.13 = (bf16[768,768]{0,1:T(8,128)(2,1)S(1)}, bf16[768,768]{0,1:T(8,128)(2,1)}, u32[]{:S(2)}) copy-start(bf16[768,768]{0,1:T(8,128)(2,1)} %copy-done.12) | copy-start | bytes 3538948
  306.3 23.7 %copy-start.45 = (s32[256]{0:T(256)S(1)}, s32[256]{0:T(256)}, u32[]{:S(2)}) copy-start(s32[256]{0:T(256)} %dynamic_slice.25) | copy-start | bytes 3076
  329.9 199.6 %reduce-scatter.9.cloned.1.call-start = ((), (), s32[]{:S(2)}) async-start(), calls=%async_computation.10 | async-start | bytes 1966080 | tf_op jit(solution)/shard_map/reduce_scatter | solution.py:56
  333.9 363.1 %reduce-scatter.11.cloned.1.call-start = ((), (), s32[]{:S(2)}) async-start(), calls=%async_computation.11 | async-start | bytes 14598144 | tf_op jit(solution)/shard_map/reduce_scatter | solution.py:191
  439.8 261.3 %copy-start.1 = (s32[4,1,1024]{2,1,0:T(1,128)S(1)}, s32[4,1,1024]{2,1,0:T(1,128)}, u32[]{:S(2)}) copy-start(s32[4,1,1024]{2,1,0:T(1,128)} %param.22) | copy-start | bytes 49156
  439.9 10.1 %all-to-all-start.1 = ((bf16[4,64,768]{2,1,0:T(8,128)(2,1)}), bf16[4,64,768]{2,1,0:T(8,128)(2,1)S(1)}, u32[]{:S(2)}, u32[]{:S(2)}) async-start(bf16[4,64,768]{2,1,0:T(8,128)(2,1)} %reduce-scatter.5.cloned.1.call-done), calls=%async_computation.2 | async-start | bytes 786432 | tf_op jit(solution)/shard_map/all_to_all | solution.py:57
  529.5 9.9 %all-to-all-start.3 = ((bf16[4,64,768]{2,1,0:T(8,128)(2,1)}), bf16[4,64,768]{2,1,0:T(8,128)(2,1)S(1)}, u32[]{:S(2)}, u32[]{:S(2)}) async-start(bf16[4,64,768]{2,1,0:T(8,128)(2,1)} %reduce-scatter.9.cloned.1.call-done), calls=%async_computation.6 | async-start | bytes 786432 | tf_op jit(solution)/shard_map/all_to_all | solution.py:57
  (53 other events, 336.0 us)
Sparse Core Ops, SparseCore 0:
  20.5 36.9 all-gather.9
  60.3 101.5 all-gather.11
  163.4 35.4 all-gather.13
  283.6 42.0 reduce-scatter.6
  327.8 35.3 reduce-scatter.4
  369.3 121.4 all-reduce.2
  493.1 36.3 reduce-scatter.8
  535.5 161.4 reduce-scatter.10
where the time goes:
time: 722 us; the launch traced here: 708 us
  waiting for transfers between devices  299 us (41%)
  local copies, waits for them, and re-layouts  189 us (26%)
  blocking collectives  103 us (14%)
  matrix products  73.7 us (10%)
  between operations  16.2 us (2%)
  other arithmetic  15.8 us (2%)
  starting transfers between devices  11.3 us (2%)
    reduce_scatter x1, waiting for transfers between devices, body(): lax.psum_scatter(packed_g, ALL, scatter_dimension=0, tiled=True)[0]  158 us
    all_gather x1, blocking collectives, body(): lax.all_gather(jnp.concatenate(bias, axis=1), ALL, axis=0, tiled=False)  68.8 us
    concatenate x2, local copies, waits for them, and re-layouts, body(): packed_g = jnp.concatenate(outs, axis=3)  52.6 us
    unnamed x9, waiting for transfers between devices  41 us
    reshape x6, local copies, waits for them, and re-layouts, body(): g.astype(BF).reshape(rows_n, width // rows_n, tp_n, wd)  37.8 us
    reduce_scatter x2, waiting for transfers between devices, scatter_group(): mine = lax.psum_scatter(blocks, 'tp', scatter_dimension=1, tiled=True)  37.3 us
    all_gather x1, waiting for transfers between devices, body(): lax.all_gather(jnp.concatenate(mats, axis=1), ALL, axis=0, tiled=False)  33.1 us
    transpose x6, local copies, waits for them, and re-layouts, body(): full.append(piece.transpose(0, 2, 1, 3).reshape(width, tp_n * wd))  27.6 us
  transfers between devices with their start and end apart: 11, of which 7 were waited for; matrix products, arithmetic and copies ran while one was open for 34% of the time, Pallas kernels for 0%

commit v1 on v0

--- a/solution.py
+++ b/solution.py
@@ -11,6 +11,18 @@
 F32 = jnp.float32
 
 
+def in_blocks(array, dim, peers):
+    dims = array.shape
+    blocks = array.reshape(*dims[:dim], peers, dims[dim] // peers, *dims[dim + 1 :])
+    return jnp.moveaxis(blocks, dim, 0)
+
+
+def laid_out(blocks, dim):
+    blocks = jnp.moveaxis(blocks, 0, dim)
+    shape = blocks.shape
+    return blocks.reshape(*shape[:dim], shape[dim] * shape[dim + 1], *shape[dim + 2 :])
+
+
 def mm(a, b):
     return jnp.dot(a, b, preferred_element_type=F32)
 
@@ -44,7 +56,14 @@
 
 def gather_group(block):
     width = block.shape[-1]
-    mine = lax.all_to_all(block, "ctx", 0, 0, tiled=True)
+    size, place = (lax.axis_size("ctx"), lax.axis_index("ctx"))
+    blocks_2 = in_blocks(block, 0, size)
+    outs_2 = [blocks_2[place]]
+    for step in range(1, size):
+        sent = blocks_2[place ^ step]
+        outs_2.append(lax.ppermute(sent, "ctx", [(i_2, i_2 ^ step) for i_2 in range(size)]))
+    blocks_2 = jnp.stack(outs_2)[place ^ jnp.arange(size)]
+    mine = laid_out(blocks_2, 0)
     whole = lax.all_gather(mine, "tp", axis=1, tiled=False)
     return whole.reshape(-1, width)
 

time: 722 us -> 704 us (0.975)
  blocking collectives: 103 us -> 89 us
    all_to_all x1 -> x0, blocking collectives: 13 us -> none  [gather_group(): mine = lax.all_to_all(block, 'ctx', 0, 0, tiled=True)]
    transpose x6, local copies, waits for them, and re-layouts: 27.6 us -> 16.8 us  [body(): full.append(piece.transpose(0, 2, 1, 3).reshape(width, tp_n * wd))]
    ppermute x0 -> x6, starting transfers between devices: none -> 8.18 us  [gather_group(): lax.ppermute(sent, 'ctx', [(i_2, i_2 ^ step) for i_2 in range(size)])]
  transfers between devices with their start and end apart: 11 -> 16, of which waited for: 7 -> 10; matrix products, arithmetic and copies ran while one was open for 34% -> 34% of each run, Pallas kernels for 0% -> 0%
where the time goes in v1:
time: 704 us; the launch traced here: 697 us
  waiting for transfers between devices  304 us (43%)
  local copies, waits for them, and re-layouts  182 us (26%)
  blocking collectives  89 us (13%)
  matrix products  73.7 us (10%)
  starting transfers between devices  16.2 us (2%)
  between operations  16.1 us (2%)
  other arithmetic  15.9 us (2%)
    reduce_scatter x1, waiting for transfers between devices, body(): lax.psum_scatter(packed_g, ALL, scatter_dimension=0, tiled=True)[0]  158 us
    all_gather x1, blocking collectives, body(): lax.all_gather(jnp.concatenate(bias, axis=1), ALL, axis=0, tiled=False)  68.4 us
    concatenate x2, local copies, waits for them, and re-layouts, body(): packed_g = jnp.concatenate(outs, axis=3)  52.6 us
    unnamed x9, waiting for transfers between devices  41 us
    reshape x6, local copies, waits for them, and re-layouts, body(): g.astype(BF).reshape(rows_n, width // rows_n, tp_n, wd)  37.8 us
    reduce_scatter x2, waiting for transfers between devices, scatter_group(): mine = lax.psum_scatter(blocks, 'tp', scatter_dimension=1, tiled=True)  37.3 us
    all_gather x1, waiting for transfers between devices, body(): lax.all_gather(jnp.concatenate(mats, axis=1), ALL, axis=0, tiled=False)  33.6 us
    dot_general x8, matrix products, mm(): return jnp.dot(a, b, preferred_element_type=F32)  26 us
  transfers between devices with their start and end apart: 16, of which 10 were waited for; matrix products, arithmetic and copies ran while one was open for 34% of the time, Pallas kernels for 0%

profile of v1, /device:TPU:0, one launch (start us, length us, event | category | flops | bytes accessed | tf_op | source)
XLA Modules:
  0.0 697.0 jit_solution(13295764174809520821)
XLA Ops:
  28.4 20.6 %all-gather.5 = bf16[8,96,6]{1,2,0:T(8,128)(2,1)S(1)} all-gather(bf16[1,96,6]{1,2,0:T(8,128)(2,1)S(1)} %bitcast.253), channel_id=1, replica_groups=mesh['fsdp'=2,'ctx'=4,'tp'=4] {'fsdp','ctx'}, dimensions={0}, use_global_device_ids=true | all-gather | bytes 10368 | tf_op jit(solution)/shard_map/all_gather | solution.py:122
  49.2 68.4 %all-gather.4 = bf16[32,3,48]{2,1,0:T(4,128)(2,1)S(1)} all-gather(bf16[1,3,48]{2,1,0:T(4,128)(2,1)S(1)} %maximum_bitcast_fusion.2), channel_id=4, replica_groups=mesh['fsdp'=2,'ctx'=4,'tp'=4] {'fsdp','ctx','tp'}, dimensions={0}, use_global_device_ids=true | all-gather | bytes 9504 | tf_op jit(solution)/shard_map/all_gather | solution.py:123
  127.5 33.6 %all-gather.12.cloned.1.call-done = bf16[3072,2304]{1,0:T(8,128)(2,1)} async-done(((bf16[96,2304]{1,0:T(8,128)(2,1)}), bf16[3072,2304]{1,0:T(8,128)(2,1)}) %all-gather.12.cloned.1.call-update) | async-done | bytes 14155792 | tf_op jit(solution)/shard_map/all_gather | solution.py:113
  161.0 8.1 %fusion.63 = (bf16[32,96,768]{2,1,0:T(8,128)(2,1)}, bf16[32,96,768]{2,1,0:T(8,128)(2,1)}) fusion(bf16[32,96,2304]{2,1,0:T(8,128)(2,1)} %bitcast.193), kind=kLoop, calls=%fused_computation.157 | loop fusion | bytes 18874368 | tf_op jit(solution)/shard_map/slice | solution.py:116
  169.2 7.1 %fusion.64 = (bf16[32,96,192]{2,1,0:T(8,128)(2,1)S(1)}, bf16[32,96,192]{2,1,0:T(8,128)(2,1)S(1)}, bf16[32,96,192]{2,1,0:T(8,128)(2,1)}, bf16[32,96,192]{2,1,0:T(8,128)(2,1)}) fusion(bf16[32,96,2304]{2,1,0:T(8,128)(2,1)} %bitcast.194), kind=kLoop, calls=%fused_computation.158 | loop fusion | bytes 9437184 | tf_op jit(solution)/shard_map/slice | solution.py:116
  215.8 6.1 fusion.69
  222.0 4.1 fusion.25
  248.5 5.0 convert_reduce_fusion
  258.3 4.0 multiply_reduce_fusion
  294.9 19.4 %reduce-scatter.7.cloned.1.call-done = f32[256,1536]{0,1:T(8,128)} async-done(((f32[512,1536]{0,1:T(8,128)}), f32[256,1536]{0,1:T(8,128)}) %reduce-scatter.7.cloned.1.call-update) | async-done | bytes 1572880 | tf_op jit(solution)/shard_map/reduce_scatter | solution.py:195
  324.4 4.4 reshape.376
  330.4 4.4 reshape.379
  334.8 5.2 convolution_convert_fusion.1
  340.0 9.9 %reshape.380 = bf16[8,96,4,768]{3,2,1,0:T(4,128)(2,1)} reshape(bf16[768,3072]{1,0:T(8,128)(2,1)} %convolution_convert_fusion.1) | data formatting | bytes 9437184 | tf_op jit(solution)/shard_map/reshape | solution.py:207
  353.6 9.8 %reshape.381 = bf16[8,96,4,768]{3,2,1,0:T(4,128)(2,1)} reshape(bf16[768,3072]{1,0:T(8,128)(2,1)} %convolution_convert_fusion) | data formatting | bytes 9437184 | tf_op jit(solution)/shard_map/reshape | solution.py:207
  364.9 4.5 reshape.377
  371.0 4.8 reshape.378
  375.8 41.4 %concatenate.27 = bf16[8,4,96,2304]{3,1,2,0:T(4,128)(2,1)} concatenate(bf16[8,4,96,192]{3,1,2,0:T(4,128)(2,1)S(1)} %bitcast.195, bf16[8,4,96,192]{3,1,2,0:T(4,128)(2,1)} %bitcast.197, bf16[8,4,96,192]{3,1,2,0:T(4,128)(2,1)} %bitcast.198, bf16[8,4,96,192]{3,1,2,0:T(4,128)(2,1)S(1)} %bitcast.196, bf16[8,4,96,768]{3,1,2,0:T(4,128)(2,1)} %bitcast.183, bf16[8,4,96,768]{3,1,2,0:T(4,128)(2,1)} %bitcast.184), dimensions={3} | concatenate | bytes 28311552 | tf_op jit(solution)/shard_map/concatenate | solution.py:208
  417.1 11.2 %copy.125 = bf16[8,4,96,2304]{3,2,1,0:T(8,128)(2,1)} copy(bf16[8,4,96,2304]{3,1,2,0:T(4,128)(2,1)} %concatenate.27) | data formatting | bytes 28311552 | tf_op jit(solution)/shard_map/concatenate | solution.py:208
  432.1 6.5 all-to-all-done
  438.6 40.9 %all-reduce.3.cloned.1.call-done = f32[32,720]{1,0:T(8,128)} async-done(((f32[32,720]{1,0:T(8,128)}), f32[32,720]{1,0:T(8,128)}) %all-reduce.3.cloned.1.call-update) | async-done | bytes 92176
  481.0 37.2 %reduce-scatter.9.cloned.1.call-done = bf16[4,64,768]{2,1,0:T(8,128)(2,1)} async-done(((bf16[4,256,768]{2,1,0:T(8,128)(2,1)}), bf16[4,64,768]{2,1,0:T(8,128)(2,1)}) %reduce-scatter.9.cloned.1.call-update) | async-done | bytes 393232 | tf_op jit(solution)/shard_map/reduce_scatter | solution.py:75
  523.9 4.1 all-to-all-done.1
  528.1 157.6 %reduce-scatter.11.cloned.1.call-done = bf16[1,96,2304]{2,1,0:T(8,128)(2,1)} async-done(((bf16[32,96,2304]{2,1,0:T(8,128)(2,1)}), bf16[1,96,2304]{2,1,0:T(8,128)(2,1)}) %reduce-scatter.11.cloned.1.call-update) | async-done | bytes 442384 | tf_op jit(solution)/shard_map/reduce_scatter | solution.py:210
  (283 shorter events, 162.5 us)
Async XLA Ops:
  7.2 114.5 %copy-start = (s32[4,1,1024]{2,1,0:T(1,128)S(1)}, s32[4,1,1024]{2,1,0:T(1,128)}, u32[]{:S(2)}) copy-start(s32[4,1,1024]{2,1,0:T(1,128)} %param.22) | copy-start | bytes 49156
  7.3 41.8 %copy-start.51 = (bf16[3,32]{1,0:T(4,128)(2,1)S(1)}, bf16[3,32]{1,0:T(4,128)(2,1)}, u32[]{:S(2)}) copy-start(bf16[3,32]{1,0:T(4,128)(2,1)} %param.33) | copy-start | bytes 580
  7.3 41.8 %copy-start.52 = (bf16[3,8]{1,0:T(4,128)(2,1)S(1)}, bf16[3,8]{1,0:T(4,128)(2,1)}, u32[]{:S(2)}) copy-start(bf16[3,8]{1,0:T(4,128)(2,1)} %param.27) | copy-start | bytes 148
  7.3 41.8 %copy-start.53 = (bf16[3,8]{1,0:T(4,128)(2,1)S(1)}, bf16[3,8]{1,0:T(4,128)(2,1)}, u32[]{:S(2)}) copy-start(bf16[3,8]{1,0:T(4,128)(2,1)} %param.24) | copy-start | bytes 148
  7.3 116.6 %all-gather.10.cloned.1.call-start = ((), (), s32[]{:S(2)}) async-start(), calls=%async_computation.10 | async-start | bytes 1966080 | tf_op jit(solution)/shard_map/all_gather | solution.py:67
  8.5 7.2 %collective-permute-start.2 = (bf16[1,64,768]{2,1,0:T(8,128)(2,1)S(1)}, bf16[1,64,768]{2,1,0:T(8,128)(2,1)S(1)}, u32[]{:S(2)}, u32[]{:S(2)}) collective-permute-start(bf16[1,64,768]{2,1,0:T(8,128)(2,1)S(1)} %get-tuple-element.55), channel_id=1, source_target_pairs={{0,12},{4,8},{8,4},{12,0},{1,13},{5,9},{9,5},{13,1},{2,14},{6,10},... | collective-permute-start | bytes 294920 | tf_op jit(solution)/shard_map/ppermute | solution.py:64
  12.5 4.9 collective-permute-start.1
  13.0 4.7 collective-permute-start
  19.1 141.9 %all-gather.12.cloned.1.call-start = ((), (), s32[]{:S(2)}) async-start(), calls=%async_computation.11 | async-start | bytes 14598144 | tf_op jit(solution)/shard_map/all_gather | solution.py:113
  21.2 223.2 %all-gather.14.cloned.1.call-start = ((), (), s32[]{:S(2)}) async-start(), calls=%async_computation.12 | async-start | bytes 1966080 | tf_op jit(solution)/shard_map/all_gather | solution.py:67
  21.3 101.0 %collective-permute-start.5 = (bf16[1,64,768]{2,1,0:T(8,128)(2,1)S(1)}, bf16[1,64,768]{2,1,0:T(8,128)(2,1)S(1)}, u32[]{:S(2)}, u32[]{:S(2)}) collective-permute-start(bf16[1,64,768]{2,1,0:T(8,128)(2,1)S(1)} %get-tuple-element.51), channel_id=1, source_target_pairs={{0,12},{4,8},{8,4},{12,0},{1,13},{5,9},{9,5},{13,1},{2,14},{6,10},... | collective-permute-start | bytes 294920 | tf_op jit(solution)/shard_map/ppermute | solution.py:64
  22.8 99.5 %collective-permute-start.4 = (bf16[1,64,768]{2,1,0:T(8,128)(2,1)S(1)}, bf16[1,64,768]{2,1,0:T(8,128)(2,1)S(1)}, u32[]{:S(2)}, u32[]{:S(2)}) collective-permute-start(bf16[1,64,768]{2,1,0:T(8,128)(2,1)S(1)} %get-tuple-element.52), channel_id=1, source_target_pairs={{0,8},{4,12},{8,0},{12,4},{1,9},{5,13},{9,1},{13,5},{2,10},{6,14},... | collective-permute-start | bytes 294920 | tf_op jit(solution)/shard_map/ppermute | solution.py:64
  24.3 98.0 %collective-permute-start.3 = (bf16[1,64,768]{2,1,0:T(8,128)(2,1)S(1)}, bf16[1,64,768]{2,1,0:T(8,128)(2,1)S(1)}, u32[]{:S(2)}, u32[]{:S(2)}) collective-permute-start(bf16[1,64,768]{2,1,0:T(8,128)(2,1)S(1)} %get-tuple-element.50), channel_id=1, source_target_pairs={{0,4},{4,0},{8,12},{12,8},{1,5},{5,1},{9,13},{13,9},{2,6},{6,2},{1... | collective-permute-start | bytes 294920 | tf_op jit(solution)/shard_map/ppermute | solution.py:64
  123.7 190.6 %reduce-scatter.7.cloned.1.call-start = ((), (), s32[]{:S(2)}) async-start(), calls=%async_computation.7 | async-start | bytes 4718592 | tf_op jit(solution)/shard_map/reduce_scatter | solution.py:195
  226.7 29.1 %copy-start.2 = (f32[256,768]{1,0:T(8,128)}, f32[256,768]{1,0:T(8,128)S(1)}, u32[]{:S(2)}) copy-start(f32[256,768]{1,0:T(8,128)S(1)} %get-tuple-element.70) | copy-start | bytes 2359300
  272.1 156.3 %reduce-scatter.5.cloned.1.call-start = ((), (), s32[]{:S(2)}) async-start(), calls=%async_computation.6 | async-start | bytes 1966080 | tf_op jit(solution)/shard_map/reduce_scatter | solution.py:75
  275.3 204.2 %all-reduce.3.cloned.1.call-start = ((), (), s32[]{:S(2)}) async-start(), calls=%async_computation.13 | async-start | bytes 196608
  292.7 23.7 %copy-start.28 = (f32[32,576]{1,0:T(8,128)S(1)}, f32[32,576]{1,0:T(8,128)}, u32[]{:S(2)}) copy-start(f32[32,576]{1,0:T(8,128)} %reshape.390) | copy-start | bytes 221188
  292.7 24.4 %copy-start.13 = (bf16[768,768]{0,1:T(8,128)(2,1)S(1)}, bf16[768,768]{0,1:T(8,128)(2,1)}, u32[]{:S(2)}) copy-start(bf16[768,768]{0,1:T(8,128)(2,1)} %copy-done.12) | copy-start | bytes 3538948
  318.5 199.6 %reduce-scatter.9.cloned.1.call-start = ((), (), s32[]{:S(2)}) async-start(), calls=%async_computation.8 | async-start | bytes 1966080 | tf_op jit(solution)/shard_map/reduce_scatter | solution.py:75
  322.5 363.1 %reduce-scatter.11.cloned.1.call-start = ((), (), s32[]{:S(2)}) async-start(), calls=%async_computation.9 | async-start | bytes 14598144 | tf_op jit(solution)/shard_map/reduce_scatter | solution.py:210
  428.4 261.5 %copy-start.1 = (s32[4,1,1024]{2,1,0:T(1,128)S(1)}, s32[4,1,1024]{2,1,0:T(1,128)}, u32[]{:S(2)}) copy-start(s32[4,1,1024]{2,1,0:T(1,128)} %param.22) | copy-start | bytes 49156
  428.4 10.2 %all-to-all-start = ((bf16[4,64,768]{2,1,0:T(8,128)(2,1)}), bf16[4,64,768]{2,1,0:T(8,128)(2,1)S(1)}, u32[]{:S(2)}, u32[]{:S(2)}) async-start(bf16[4,64,768]{2,1,0:T(8,128)(2,1)} %reduce-scatter.5.cloned.1.call-done), calls=%async_computation.1 | async-start | bytes 786432 | tf_op jit(solution)/shard_map/all_to_all | solution.py:76
  518.2 9.9 %all-to-all-start.1 = ((bf16[4,64,768]{2,1,0:T(8,128)(2,1)}), bf16[4,64,768]{2,1,0:T(8,128)(2,1)S(1)}, u32[]{:S(2)}, u32[]{:S(2)}) async-start(bf16[4,64,768]{2,1,0:T(8,128)(2,1)} %reduce-scatter.9.cloned.1.call-done), calls=%async_computation.4 | async-start | bytes 786432 | tf_op jit(solution)/shard_map/all_to_all | solution.py:76
  (58 other events, 444.7 us)
Sparse Core Ops, SparseCore 0:
  19.3 37.4 all-gather.9
  59.5 101.4 all-gather.11
  162.6 35.4 all-gather.13
  272.3 42.0 reduce-scatter.6
  316.5 35.4 reduce-scatter.4
  358.0 121.4 all-reduce.2
  481.8 36.3 reduce-scatter.8
  524.2 161.4 reduce-scatter.10
